TPU v7x, 32 devices: a whole 2x2x4 slice. The times are simulated.
32 devices in a mesh: sp: 8 (over z, x), tp: 4 (over y, core).
Axes of the slice: x: 2, y: 2, z: 4, core: 2. Of those that a mesh axis runs over, the one named last changes fastest.
Arguments:
- prefill_keys: bfloat16 [2, 8, 512, 8, 128], P(None, None, 'sp', 'tp'), may hold values from -6 to 6
- prefill_values: bfloat16 [2, 8, 512, 8, 128], P(None, None, 'sp', 'tp'), may hold values from -6 to 6
- prompt_lengths: int32 [8], replicated, may hold values from 1 to 512, 2048 in all
- destination: int32 [8], replicated, may hold values from 0 to 7, each once
- page_table: int32 [8, 32], P('sp'), may hold values from 0 to 31, as said below
- queries: bfloat16 [2, 8, 64, 128], P(None, 'sp', 'tp'), may hold values from -6 to 6
Outputs:
- key_pages: bfloat16 [2, 256, 16, 8, 128], P(None, 'sp', None, 'tp')
- value_pages: bfloat16 [2, 256, 16, 8, 128], P(None, 'sp', None, 'tp')
- attended: bfloat16 [2, 8, 64, 128], P(None, 'sp')
Inputs may be any that keep to these rules, and one draw needn't show every extreme that they name: `destination`: each slot is named by exactly one prompt; slot s is held by sp index s // 1. `page_table`: the rows of the 1 slots of one sp index together name each of that index's 1 times 32 local pool pages exactly once.
All inputs are finite; a program needn't handle non-finite values.
Results may differ from a plain program's by a relative error of at most 0.0085.
Values may be sent and summed in bfloat16 or wider, within the bound.
A program may use at most 128 MiB of HBM per device.

v0:
```python
import jax
import jax.numpy as jnp
from jax import lax
from jax.sharding import PartitionSpec as P


def local(prefill_keys, prefill_values, prompt_lengths, destination, page_table, queries):
    layers = prefill_keys.shape[0]
    prompts = prefill_keys.shape[1]
    heads_here = prefill_keys.shape[3]
    head_size = prefill_keys.shape[4]
    prompt_ids = jnp.arange(prompts, dtype=jnp.int32)
    chooser = destination[None, :] == prompt_ids[:, None]
    holder = jnp.sum(jnp.where(chooser, prompt_ids[None, :], 0), axis=1).astype(jnp.int32)
    chooser_mat = chooser.astype(jnp.bfloat16)
    sorted_keys = jnp.einsum(
        "sp,lptkd->lstkd", chooser_mat, prefill_keys, preferred_element_type=jnp.float32
    ).astype(jnp.bfloat16)
    sorted_values = jnp.einsum(
        "sp,lptkd->lstkd", chooser_mat, prefill_values, preferred_element_type=jnp.float32
    ).astype(jnp.bfloat16)
    seq_keys, seq_values = (
        lax.all_to_all(sorted_keys, "sp", split_axis=1, concat_axis=2, tiled=True),
        lax.all_to_all(sorted_values, "sp", split_axis=1, concat_axis=2, tiled=True),
    )
    slots_here = page_table.shape[0]
    pages_each = page_table.shape[1]
    max_len = seq_keys.shape[2]
    page_size = max_len // pages_each
    first_slot = lax.axis_index("sp") * slots_here
    my_holder = lax.dynamic_slice_in_dim(holder, first_slot, slots_here)
    my_len = jnp.sum(
        jnp.where(prompt_ids[None, :] == my_holder[:, None], prompt_lengths[None, :], 0), axis=1
    ).astype(jnp.int32)
    positions = jnp.arange(max_len, dtype=jnp.int32)
    inside = positions[None, :] < my_len[:, None]
    seq_keys = jnp.where(inside[None, :, :, None, None], seq_keys, 0).astype(seq_keys.dtype)
    seq_values = jnp.where(inside[None, :, :, None, None], seq_values, 0).astype(seq_values.dtype)
    local_pages = slots_here * pages_each
    block_shape = (layers, local_pages, page_size, heads_here, head_size)
    page_order = page_table.reshape(-1)
    placing = (page_order[:, None] == jnp.arange(local_pages, dtype=jnp.int32)[None, :]).astype(
        jnp.bfloat16
    )
    key_blocks = seq_keys.reshape(block_shape)
    value_blocks = seq_values.reshape(block_shape)
    key_pages = jnp.einsum(
        "iq,liokd->lqokd", placing, key_blocks, preferred_element_type=jnp.float32
    ).astype(jnp.bfloat16)
    value_pages = jnp.einsum(
        "iq,liokd->lqokd", placing, value_blocks, preferred_element_type=jnp.float32
    ).astype(jnp.bfloat16)
    seq_shape = (layers, slots_here, max_len, heads_here, head_size)
    read_keys = (
        jnp.einsum("iq,lqokd->liokd", placing, key_pages, preferred_element_type=jnp.float32)
        .astype(jnp.bfloat16)
        .reshape(seq_shape)
    )
    read_values = (
        jnp.einsum("iq,lqokd->liokd", placing, value_pages, preferred_element_type=jnp.float32)
        .astype(jnp.bfloat16)
        .reshape(seq_shape)
    )
    query_heads = queries.shape[2]
    groups = query_heads // heads_here
    score_scale = head_size ** (-0.5)
    grouped = queries.reshape(layers, slots_here, heads_here, groups, head_size)
    scores = (
        jnp.einsum("lpkgd,lptkd->lpkgt", grouped, read_keys, preferred_element_type=jnp.float32)
        * score_scale
    )
    scores = jnp.where(inside[None, :, None, None, :], scores, -1e30)
    weights = jax.nn.softmax(scores, axis=-1)
    output = jnp.einsum("lpkgt,lptkd->lpkgd", weights, read_values.astype(jnp.float32))
    output = output.reshape(layers, slots_here, query_heads, head_size).astype(jnp.bfloat16)
    attended = lax.all_gather(output, "tp", axis=2, tiled=True)
    return (key_pages, value_pages, attended)


def solution(mesh):
    placed = (
        P(None, None, "sp", "tp", None),
        P(None, None, "sp", "tp", None),
        P(),
        P(),
        P("sp", None),
        P(None, "sp", "tp", None),
    )
    return jax.shard_map(
        local,
        mesh=mesh,
        in_specs=placed,
        out_specs=(
            P(None, "sp", None, "tp", None),
            P(None, "sp", None, "tp", None),
            P(None, "sp", None, None),
        ),
        check_vma=False,
    )
```

profile of v0, /device:TPU:0, one launch (start us, length us, event | category | flops | bytes accessed | tf_op | source)
XLA Modules:
  0.0 56.7 jit_solution(9429967539409540372)
XLA Ops:
  0.6 1.0 %copy-done = bf16[2,8,64,2,128]{4,3,2,1,0:T(2,128)(2,1)S(1)} copy-done((bf16[2,8,64,2,128]{4,3,2,1,0:T(2,128)(2,1)S(1)}, bf16[2,8,64,2,128]{4,3,2,1,0:T(2,128)(2,1)}, u32[]{:S(2)}) %copy-start) | copy-done | bytes 524312
  1.7 1.1 %fusion = bf16[2,8,64,2,128]{4,1,3,2,0:T(8,128)(2,1)S(1)} fusion(bf16[2,8,64,2,128]{4,3,2,1,0:T(2,128)(2,1)S(1)} %copy-done, s32[8]{0:T(128)} %param.9), kind=kOutput, calls=%fused_computation.6 | convolution fusion | flops 4456512 | bytes 1048608 | tf_op jit(solution)/shard_map/sp,lptkd->lstkd/dot_general | solution.py:16
  2.7 1.3 %copy.30 = bf16[2,8,64,2,128]{4,3,2,0,1:T(2,128)(2,1)} copy(bf16[2,8,64,2,128]{4,1,3,2,0:T(8,128)(2,1)S(1)} %fusion) | data formatting | bytes 1048576 | tf_op jit(solution)/shard_map/convert_element_type | solution.py:18
  4.0 7.4 %all-to-all-start = ((bf16[2,8,64,2,128]{4,3,2,0,1:T(2,128)(2,1)}), bf16[2,8,64,2,128]{4,3,2,0,1:T(2,128)(2,1)S(1)}, u32[]{:S(2)}, u32[]{:S(2)}) async-start(bf16[2,8,64,2,128]{4,3,2,0,1:T(2,128)(2,1)} %copy.30), calls=%async_computation | async-start | bytes 1048576 | tf_op jit(solution)/shard_map/all_to_all | solution.py:23
  11.4 0.4 fusion.1
  11.8 1.3 %copy.35 = bf16[2,8,64,2,128]{4,3,2,0,1:T(2,128)(2,1)} copy(bf16[2,8,64,2,128]{4,1,3,2,0:T(8,128)(2,1)S(1)} %fusion.1) | data formatting | bytes 1048576 | tf_op jit(solution)/shard_map/convert_element_type | solution.py:21
  13.1 12.8 %all-to-all-done = bf16[2,8,64,2,128]{4,3,2,0,1:T(2,128)(2,1)S(1)} async-done(((bf16[2,8,64,2,128]{4,3,2,0,1:T(2,128)(2,1)}), bf16[2,8,64,2,128]{4,3,2,0,1:T(2,128)(2,1)S(1)}, u32[]{:S(2)}, u32[]{:S(2)}) %all-to-all-start) | async-done | bytes 524320 | tf_op jit(solution)/shard_map/all_to_all | solution.py:23
  25.9 3.6 %all-to-all-start.1 = ((bf16[2,8,64,2,128]{4,3,2,0,1:T(2,128)(2,1)}), bf16[2,8,64,2,128]{4,3,2,0,1:T(2,128)(2,1)S(1)}, u32[]{:S(2)}, u32[]{:S(2)}) async-start(bf16[2,8,64,2,128]{4,3,2,0,1:T(2,128)(2,1)} %copy.35), calls=%async_computation.1 | async-start | bytes 1048576 | tf_op jit(solution)/shard_map/all_to_all | solution.py:24
  29.5 0.1 select_reduce_fusion
  29.7 0.6 %dynamic_slice.3 = s32[1]{0:T(128)} dynamic-slice(s32[8]{0:T(128)S(1)} %select_reduce_fusion, s32[]{:T(128)S(6)} %select_n.34), dynamic_slice_sizes={1} | dynamic-slice | bytes 12 | tf_op jit(solution)/shard_map/dynamic_slice | solution.py:31
  30.2 0.7 %copy-done.5 = s32[8]{0:T(128)S(1)} copy-done((s32[8]{0:T(128)S(1)}, s32[8]{0:T(128)}, u32[]{:S(2)}) %copy-start.5) | copy-done | bytes 56
  30.9 1.3 %fusion.32 = s32[]{:T(128)} fusion(s32[8]{0:T(128)S(1)} %copy-done.5, s32[]{:T(128)} %bitcast), kind=kLoop, calls=%fused_computation.43 | loop fusion | flops 23 | bytes 40 | tf_op jit(solution)/shard_map/reduce_sum | solution.py:32
  32.2 0.6 %iota_compare_fusion.2 = pred[512]{0:T(512)(128)(4,1)S(1)} fusion(s32[]{:T(128)} %fusion.32), kind=kLoop, calls=%fused_computation.39 | loop fusion | flops 512 | bytes 516 | tf_op jit(solution)/shard_map/lt | solution.py:36
  32.8 0.7 %add_compare_fusion = pred[32,16]{1,0:T(8,128)(4,1)S(1)} fusion(s32[]{:T(128)} %fusion.32), kind=kLoop, calls=%fused_computation.29 | loop fusion | flops 1536 | bytes 516 | tf_op jit(solution)/shard_map/lt | solution.py:36
  33.5 0.1 copy.31
  33.6 10.6 %all-to-all-done.1 = bf16[2,8,64,2,128]{4,3,2,0,1:T(2,128)(2,1)S(1)} async-done(((bf16[2,8,64,2,128]{4,3,2,0,1:T(2,128)(2,1)}), bf16[2,8,64,2,128]{4,3,2,0,1:T(2,128)(2,1)S(1)}, u32[]{:S(2)}, u32[]{:S(2)}) %all-to-all-start.1) | async-done | bytes 524320 | tf_op jit(solution)/shard_map/all_to_all | solution.py:24
  44.3 0.1 broadcast_select_fusion
  44.5 0.6 %copy-done.3 = s32[1,32]{1,0:T(1,128)S(1)} copy-done((s32[1,32]{1,0:T(1,128)S(1)}, s32[1,32]{1,0:T(1,128)}, u32[]{:S(2)}) %copy-start.3) | copy-done | bytes 152
  45.1 0.4 fusion.2
  45.6 1.2 %copy.42 = bf16[2,32,16,2,128]{4,3,2,1,0:T(2,128)(2,1)} copy(bf16[2,32,16,2,128]{4,1,3,2,0:T(8,128)(2,1)S(1)} %fusion.2) | data formatting | bytes 1048576
  46.8 0.3 fusion.4
  47.1 0.4 fusion.3
  47.5 1.2 %copy.43 = bf16[2,32,16,2,128]{4,3,2,1,0:T(2,128)(2,1)} copy(bf16[2,32,16,2,128]{4,1,3,2,0:T(8,128)(2,1)S(1)} %fusion.3) | data formatting | bytes 1048576
  48.7 0.3 fusion.5
  49.1 0.3 copy.39
  49.5 0.3 copy.40
  49.8 0.3 copy-done.2
  50.1 0.3 fusion.33
  50.5 0.2 fusion.14
  50.7 0.2 fusion.8
  50.9 5.2 %all_gather.3 = bf16[2,1,64,128]{3,2,1,0:T(8,128)(2,1)S(1)} all-gather(bf16[2,1,16,128]{3,2,1,0:T(8,128)(2,1)S(1)} %fusion.8), channel_id=1, replica_groups=mesh['sp'=8,'tp'=4] {'tp'}, dimensions={2}, use_global_device_ids=true | all-gather | bytes 40960 | tf_op jit(solution)/shard_map/all_gather | solution.py:76
  56.1 0.6 %copy.59 = bf16[2,1,64,128]{3,2,1,0:T(8,128)(2,1)} copy(bf16[2,1,64,128]{3,2,1,0:T(8,128)(2,1)S(1)} %all_gather.3) | data formatting | bytes 65536
  (9 shorter events, 0.1 us)
Async XLA Ops:
  0.6 1.0 %copy-start = (bf16[2,8,64,2,128]{4,3,2,1,0:T(2,128)(2,1)S(1)}, bf16[2,8,64,2,128]{4,3,2,1,0:T(2,128)(2,1)}, u32[]{:S(2)}) copy-start(bf16[2,8,64,2,128]{4,3,2,1,0:T(2,128)(2,1)} %param.6) | copy-start | bytes 1572868
  4.0 7.4 %copy-start.1 = (bf16[2,8,64,2,128]{4,3,2,1,0:T(2,128)(2,1)S(1)}, bf16[2,8,64,2,128]{4,3,2,1,0:T(2,128)(2,1)}, u32[]{:S(2)}) copy-start(bf16[2,8,64,2,128]{4,3,2,1,0:T(2,128)(2,1)} %param.7) | copy-start | bytes 1572868
  4.0 7.4 %copy-start.4 = (s32[8]{0:T(128)S(1)}, s32[8]{0:T(128)}, u32[]{:S(2)}) copy-start(s32[8]{0:T(128)} %param.9) | copy-start | bytes 100
  4.0 21.9 %all-to-all-start = ((bf16[2,8,64,2,128]{4,3,2,0,1:T(2,128)(2,1)}), bf16[2,8,64,2,128]{4,3,2,0,1:T(2,128)(2,1)S(1)}, u32[]{:S(2)}, u32[]{:S(2)}) async-start(bf16[2,8,64,2,128]{4,3,2,0,1:T(2,128)(2,1)} %copy.30), calls=%async_computation | async-start | bytes 1048576 | tf_op jit(solution)/shard_map/all_to_all | solution.py:23
  25.9 18.3 %all-to-all-start.1 = ((bf16[2,8,64,2,128]{4,3,2,0,1:T(2,128)(2,1)}), bf16[2,8,64,2,128]{4,3,2,0,1:T(2,128)(2,1)S(1)}, u32[]{:S(2)}, u32[]{:S(2)}) async-start(bf16[2,8,64,2,128]{4,3,2,0,1:T(2,128)(2,1)} %copy.35), calls=%async_computation.1 | async-start | bytes 1048576 | tf_op jit(solution)/shard_map/all_to_all | solution.py:24
  30.2 0.7 %copy-start.5 = (s32[8]{0:T(128)S(1)}, s32[8]{0:T(128)}, u32[]{:S(2)}) copy-start(s32[8]{0:T(128)} %param.8) | copy-start | bytes 100
  44.5 0.7 %copy-start.3 = (s32[1,32]{1,0:T(1,128)S(1)}, s32[1,32]{1,0:T(1,128)}, u32[]{:S(2)}) copy-start(s32[1,32]{1,0:T(1,128)} %param.10) | copy-start | bytes 388
  49.4 0.7 %copy-start.2 = (bf16[2,1,16,128]{3,2,1,0:T(8,128)(2,1)S(1)}, bf16[2,1,16,128]{3,2,1,0:T(8,128)(2,1)}, u32[]{:S(2)}) copy-start(bf16[2,1,16,128]{3,2,1,0:T(8,128)(2,1)} %param.11) | copy-start | bytes 24580
where the time goes:
time: 57.1 us; the launch traced here: 56.7 us
  waiting for transfers between devices  23.4 us (41%)
  starting transfers between devices  11 us (19%)
  local copies, waits for them, and re-layouts  9.74 us (17%)
  blocking collectives  5.19 us (9%)
  matrix products  3.54 us (6%)
  other arithmetic  3.03 us (5%)
  between operations  0.76 us (1%)
    all_to_all x1, waiting for transfers between devices, local(): lax.all_to_all(sorted_keys, 'sp', split_axis=1, concat_axis=2, tiled=True)  12.8 us
    all_to_all x1, waiting for transfers between devices, local(): lax.all_to_all(sorted_values, 'sp', split_axis=1, concat_axis=2, tiled=True)  10.6 us
    all_to_all x1, starting transfers between devices, local(): lax.all_to_all(sorted_keys, 'sp', split_axis=1, concat_axis=2, tiled=True)  7.41 us
    unnamed x15, local copies, waits for them, and re-layouts  5.71 us
    all_gather x1, blocking collectives, local(): attended = lax.all_gather(output, 'tp', axis=2, tiled=True)  5.19 us
    all_to_all x1, starting transfers between devices, local(): lax.all_to_all(sorted_values, 'sp', split_axis=1, concat_axis=2, tiled=True)  3.64 us
    lt x2, other arithmetic, local(): inside = positions[None, :] < my_len[:, None]  1.31 us
    reduce_sum x1, other arithmetic, local(): jnp.sum(jnp.where(prompt_ids[None, :] == my_holder[:, None], prompt_lengt...  1.27 us
  transfers between devices with their start and end apart: 2, of which 2 were waited for; matrix products, arithmetic and copies ran while one was open for 9% of the time, Pallas kernels for 0%

commit v1 on v0

--- a/solution.py
+++ b/solution.py
@@ -73,7 +73,12 @@
     weights = jax.nn.softmax(scores, axis=-1)
     output = jnp.einsum("lpkgt,lptkd->lpkgd", weights, read_values.astype(jnp.float32))
     output = output.reshape(layers, slots_here, query_heads, head_size).astype(jnp.bfloat16)
-    attended = lax.all_gather(output, "tp", axis=2, tiled=True)
+    ring = [output]
+    for hop in range(3):
+        ring.append(lax.ppermute(ring[-1], "tp", [(dev, (dev + 1) % 4) for dev in range(4)]))
+    attended = jnp.roll(
+        jnp.concatenate(ring[::-1], axis=2), (lax.axis_index("tp") + 1) * ring[0].shape[2], axis=2
+    )
     return (key_pages, value_pages, attended)
 
 

time: 57.1 us -> 59.4 us (1.040)
  waiting for transfers between devices: 23.4 us -> 30.2 us
  blocking collectives: 5.19 us -> 0 us
    ppermute x0 -> x3, waiting for transfers between devices: none -> 6.81 us  [local(): lax.ppermute(ring[-1], 'tp', [(dev, (dev + 1) % 4) for dev in range(4)])]
    all_gather x1 -> x0, blocking collectives: 5.19 us -> none  [local(): attended = lax.all_gather(output, 'tp', axis=2, tiled=True)]
    dynamic_slice x0 -> x1, local copies, waits for them, and re-layouts: none -> 0.63 us  [local(): jnp.roll(jnp.concatenate(ring[::-1], axis=2), (lax.axis_index('tp') + 1)...]
    unnamed x15 -> x21, local copies, waits for them, and re-layouts: 5.71 us -> 5.14 us
  transfers between devices with their start and end apart: 2 -> 5, of which waited for: 2 -> 5; matrix products, arithmetic and copies ran while one was open for 9% -> 13% of each run, Pallas kernels for 0% -> 0%
where the time goes in v1:
time: 59.4 us; the launch traced here: 58.5 us
  waiting for transfers between devices  30.2 us (51%)
  starting transfers between devices  11.1 us (19%)
  local copies, waits for them, and re-layouts  9.81 us (17%)
  matrix products  3.53 us (6%)
  other arithmetic  3.03 us (5%)
  between operations  0.78 us (1%)
    all_to_all x1, waiting for transfers between devices, local(): lax.all_to_all(sorted_keys, 'sp', split_axis=1, concat_axis=2, tiled=True)  12.8 us
    all_to_all x1, waiting for transfers between devices, local(): lax.all_to_all(sorted_values, 'sp', split_axis=1, concat_axis=2, tiled=True)  10.6 us
    all_to_all x1, starting transfers between devices, local(): lax.all_to_all(sorted_keys, 'sp', split_axis=1, concat_axis=2, tiled=True)  7.41 us
    ppermute x3, waiting for transfers between devices, local(): lax.ppermute(ring[-1], 'tp', [(dev, (dev + 1) % 4) for dev in range(4)])  6.81 us
    unnamed x21, local copies, waits for them, and re-layouts  5.14 us
    all_to_all x1, starting transfers between devices, local(): lax.all_to_all(sorted_values, 'sp', split_axis=1, concat_axis=2, tiled=True)  3.64 us
    lt x2, other arithmetic, local(): inside = positions[None, :] < my_len[:, None]  1.31 us
    reduce_sum x1, other arithmetic, local(): jnp.sum(jnp.where(prompt_ids[None, :] == my_holder[:, None], prompt_lengt...  1.27 us
  transfers between devices with their start and end apart: 5, of which 5 were waited for; matrix products, arithmetic and copies ran while one was open for 13% of the time, Pallas kernels for 0%

profile of v1, /device:TPU:0, one launch (start us, length us, event | category | flops | bytes accessed | tf_op | source)
XLA Modules:
  0.0 58.5 jit_solution(16001728083668961178)
XLA Ops:
  0.6 1.0 %copy-done = bf16[2,8,64,2,128]{4,3,2,1,0:T(2,128)(2,1)S(1)} copy-done((bf16[2,8,64,2,128]{4,3,2,1,0:T(2,128)(2,1)S(1)}, bf16[2,8,64,2,128]{4,3,2,1,0:T(2,128)(2,1)}, u32[]{:S(2)}) %copy-start) | copy-done | bytes 524312
  1.7 1.1 %fusion = bf16[2,8,64,2,128]{4,1,3,2,0:T(8,128)(2,1)S(1)} fusion(bf16[2,8,64,2,128]{4,3,2,1,0:T(2,128)(2,1)S(1)} %copy-done, s32[8]{0:T(128)} %param.9), kind=kOutput, calls=%fused_computation.6 | convolution fusion | flops 4456512 | bytes 1048608 | tf_op jit(solution)/shard_map/sp,lptkd->lstkd/dot_general | solution.py:16
  2.7 1.3 %copy.34 = bf16[2,8,64,2,128]{4,3,2,0,1:T(2,128)(2,1)} copy(bf16[2,8,64,2,128]{4,1,3,2,0:T(8,128)(2,1)S(1)} %fusion) | data formatting | bytes 1048576 | tf_op jit(solution)/shard_map/convert_element_type | solution.py:18
  4.0 7.4 %all-to-all-start = ((bf16[2,8,64,2,128]{4,3,2,0,1:T(2,128)(2,1)}), bf16[2,8,64,2,128]{4,3,2,0,1:T(2,128)(2,1)S(1)}, u32[]{:S(2)}, u32[]{:S(2)}) async-start(bf16[2,8,64,2,128]{4,3,2,0,1:T(2,128)(2,1)} %copy.34), calls=%async_computation | async-start | bytes 1048576 | tf_op jit(solution)/shard_map/all_to_all | solution.py:23
  11.4 0.4 fusion.1
  11.8 1.3 %copy.39 = bf16[2,8,64,2,128]{4,3,2,0,1:T(2,128)(2,1)} copy(bf16[2,8,64,2,128]{4,1,3,2,0:T(8,128)(2,1)S(1)} %fusion.1) | data formatting | bytes 1048576 | tf_op jit(solution)/shard_map/convert_element_type | solution.py:21
  13.1 12.8 %all-to-all-done = bf16[2,8,64,2,128]{4,3,2,0,1:T(2,128)(2,1)S(1)} async-done(((bf16[2,8,64,2,128]{4,3,2,0,1:T(2,128)(2,1)}), bf16[2,8,64,2,128]{4,3,2,0,1:T(2,128)(2,1)S(1)}, u32[]{:S(2)}, u32[]{:S(2)}) %all-to-all-start) | async-done | bytes 524320 | tf_op jit(solution)/shard_map/all_to_all | solution.py:23
  25.9 3.6 %all-to-all-start.1 = ((bf16[2,8,64,2,128]{4,3,2,0,1:T(2,128)(2,1)}), bf16[2,8,64,2,128]{4,3,2,0,1:T(2,128)(2,1)S(1)}, u32[]{:S(2)}, u32[]{:S(2)}) async-start(bf16[2,8,64,2,128]{4,3,2,0,1:T(2,128)(2,1)} %copy.39), calls=%async_computation.1 | async-start | bytes 1048576 | tf_op jit(solution)/shard_map/all_to_all | solution.py:24
  29.7 0.6 %dynamic_slice.7 = s32[1]{0:T(128)} dynamic-slice(s32[8]{0:T(128)S(1)} %select_reduce_fusion, s32[]{:T(128)S(6)} %select_n.47), dynamic_slice_sizes={1} | dynamic-slice | bytes 12 | tf_op jit(solution)/shard_map/dynamic_slice | solution.py:31
  30.2 0.7 %copy-done.5 = s32[8]{0:T(128)S(1)} copy-done((s32[8]{0:T(128)S(1)}, s32[8]{0:T(128)}, u32[]{:S(2)}) %copy-start.5) | copy-done | bytes 56
  30.9 1.3 %fusion.32 = s32[]{:T(128)} fusion(s32[8]{0:T(128)S(1)} %copy-done.5, s32[]{:T(128)} %bitcast), kind=kLoop, calls=%fused_computation.51 | loop fusion | flops 23 | bytes 40 | tf_op jit(solution)/shard_map/reduce_sum | solution.py:32
  32.2 0.6 %iota_compare_fusion.2 = pred[512]{0:T(512)(128)(4,1)S(1)} fusion(s32[]{:T(128)} %fusion.32), kind=kLoop, calls=%fused_computation.47 | loop fusion | flops 512 | bytes 516 | tf_op jit(solution)/shard_map/lt | solution.py:36
  32.8 0.7 %add_compare_fusion = pred[32,16]{1,0:T(8,128)(4,1)S(1)} fusion(s32[]{:T(128)} %fusion.32), kind=kLoop, calls=%fused_computation.37 | loop fusion | flops 1536 | bytes 516 | tf_op jit(solution)/shard_map/lt | solution.py:36
  33.6 10.6 %all-to-all-done.1 = bf16[2,8,64,2,128]{4,3,2,0,1:T(2,128)(2,1)S(1)} async-done(((bf16[2,8,64,2,128]{4,3,2,0,1:T(2,128)(2,1)}), bf16[2,8,64,2,128]{4,3,2,0,1:T(2,128)(2,1)S(1)}, u32[]{:S(2)}, u32[]{:S(2)}) %all-to-all-start.1) | async-done | bytes 524320 | tf_op jit(solution)/shard_map/all_to_all | solution.py:24
  44.3 0.1 broadcast_select_fusion
  44.5 0.6 %copy-done.3 = s32[1,32]{1,0:T(1,128)S(1)} copy-done((s32[1,32]{1,0:T(1,128)S(1)}, s32[1,32]{1,0:T(1,128)}, u32[]{:S(2)}) %copy-start.3) | copy-done | bytes 152
  45.1 0.4 fusion.3
  45.6 0.4 fusion.2
  46.0 0.3 fusion.4
  46.3 0.3 copy.43
  46.7 0.3 fusion.5
  47.1 0.3 copy.44
  47.4 0.3 copy-done.2
  47.7 0.3 fusion.33
  48.1 0.2 fusion.14
  48.3 0.2 fusion.8
  48.5 3.1 %collective-permute-done = bf16[2,1,16,128]{3,2,1,0:T(8,128)(2,1)S(1)} collective-permute-done((bf16[2,1,16,128]{3,2,1,0:T(8,128)(2,1)S(1)}, bf16[2,1,16,128]{3,2,1,0:T(8,128)(2,1)S(1)}, u32[]{:S(2)}, u32[]{:S(2)}) %collective-permute-start) | collective-permute-done | bytes 8224 | tf_op jit(solution)/shard_map/ppermute | solution.py:78
  51.6 3.1 %collective-permute-done.1 = bf16[2,1,16,128]{3,2,1,0:T(8,128)(2,1)S(1)} collective-permute-done((bf16[2,1,16,128]{3,2,1,0:T(8,128)(2,1)S(1)}, bf16[2,1,16,128]{3,2,1,0:T(8,128)(2,1)S(1)}, u32[]{:S(2)}, u32[]{:S(2)}) %collective-permute-start.1) | collective-permute-done | bytes 8224 | tf_op jit(solution)/shard_map/ppermute | solution.py:78
  54.7 1.2 %copy.48 = bf16[2,32,16,2,128]{4,3,2,1,0:T(2,128)(2,1)} copy(bf16[2,32,16,2,128]{4,1,3,2,0:T(8,128)(2,1)S(1)} %fusion.2) | data formatting | bytes 1048576
  55.9 1.2 %copy.49 = bf16[2,32,16,2,128]{4,3,2,1,0:T(2,128)(2,1)} copy(bf16[2,32,16,2,128]{4,1,3,2,0:T(8,128)(2,1)S(1)} %fusion.3) | data formatting | bytes 1048576
  57.1 0.7 %collective-permute-done.2 = bf16[2,1,16,128]{3,2,1,0:T(8,128)(2,1)S(1)} collective-permute-done((bf16[2,1,16,128]{3,2,1,0:T(8,128)(2,1)S(1)}, bf16[2,1,16,128]{3,2,1,0:T(8,128)(2,1)S(1)}, u32[]{:S(2)}, u32[]{:S(2)}) %collective-permute-start.2) | collective-permute-done | bytes 8224 | tf_op jit(solution)/shard_map/ppermute | solution.py:78
  57.8 0.6 %constant_dynamic-slice_fusion = bf16[2,1,64,128]{3,2,1,0:T(8,128)(2,1)} fusion(bf16[2,1,128,128]{3,2,1,0:T(8,128)(2,1)S(1)} %constant_dynamic-update-slice_fusion, s32[]{:T(128)S(6)} %select_n.54), kind=kLoop, calls=%fused_computation.52 | loop fusion | bytes 65540 | tf_op jit(solution)/shard_map/jit(_roll_dynamic)/dynamic_slice | solution.py:79
  (22 shorter events, 0.5 us)
Async XLA Ops:
  0.6 1.0 %copy-start = (bf16[2,8,64,2,128]{4,3,2,1,0:T(2,128)(2,1)S(1)}, bf16[2,8,64,2,128]{4,3,2,1,0:T(2,128)(2,1)}, u32[]{:S(2)}) copy-start(bf16[2,8,64,2,128]{4,3,2,1,0:T(2,128)(2,1)} %param.6) | copy-start | bytes 1572868
  4.0 7.4 %copy-start.1 = (bf16[2,8,64,2,128]{4,3,2,1,0:T(2,128)(2,1)S(1)}, bf16[2,8,64,2,128]{4,3,2,1,0:T(2,128)(2,1)}, u32[]{:S(2)}) copy-start(bf16[2,8,64,2,128]{4,3,2,1,0:T(2,128)(2,1)} %param.7) | copy-start | bytes 1572868
  4.0 7.4 %copy-start.4 = (s32[8]{0:T(128)S(1)}, s32[8]{0:T(128)}, u32[]{:S(2)}) copy-start(s32[8]{0:T(128)} %param.9) | copy-start | bytes 100
  4.0 21.9 %all-to-all-start = ((bf16[2,8,64,2,128]{4,3,2,0,1:T(2,128)(2,1)}), bf16[2,8,64,2,128]{4,3,2,0,1:T(2,128)(2,1)S(1)}, u32[]{:S(2)}, u32[]{:S(2)}) async-start(bf16[2,8,64,2,128]{4,3,2,0,1:T(2,128)(2,1)} %copy.34), calls=%async_computation | async-start | bytes 1048576 | tf_op jit(solution)/shard_map/all_to_all | solution.py:23
  25.9 18.3 %all-to-all-start.1 = ((bf16[2,8,64,2,128]{4,3,2,0,1:T(2,128)(2,1)}), bf16[2,8,64,2,128]{4,3,2,0,1:T(2,128)(2,1)S(1)}, u32[]{:S(2)}, u32[]{:S(2)}) async-start(bf16[2,8,64,2,128]{4,3,2,0,1:T(2,128)(2,1)} %copy.39), calls=%async_computation.1 | async-start | bytes 1048576 | tf_op jit(solution)/shard_map/all_to_all | solution.py:24
  30.2 0.7 %copy-start.5 = (s32[8]{0:T(128)S(1)}, s32[8]{0:T(128)}, u32[]{:S(2)}) copy-start(s32[8]{0:T(128)} %param.8) | copy-start | bytes 100
  44.5 0.7 %copy-start.3 = (s32[1,32]{1,0:T(1,128)S(1)}, s32[1,32]{1,0:T(1,128)}, u32[]{:S(2)}) copy-start(s32[1,32]{1,0:T(1,128)} %param.10) | copy-start | bytes 388
  47.0 0.7 %copy-start.2 = (bf16[2,1,16,128]{3,2,1,0:T(8,128)(2,1)S(1)}, bf16[2,1,16,128]{3,2,1,0:T(8,128)(2,1)}, u32[]{:S(2)}) copy-start(bf16[2,1,16,128]{3,2,1,0:T(8,128)(2,1)} %param.11) | copy-start | bytes 24580
  48.5 3.1 %collective-permute-start = (bf16[2,1,16,128]{3,2,1,0:T(8,128)(2,1)S(1)}, bf16[2,1,16,128]{3,2,1,0:T(8,128)(2,1)S(1)}, u32[]{:S(2)}, u32[]{:S(2)}) collective-permute-start(bf16[2,1,16,128]{3,2,1,0:T(8,128)(2,1)S(1)} %fusion.8), channel_id=1, source_target_pairs={{0,1},{1,2},{2,3},{3,0},{4,5},{5,6},{6,7},{7,4},{8,9},{9,10},{10,1... | collective-permute-start | bytes 24584 | tf_op jit(solution)/shard_map/ppermute | solution.py:78
  51.6 3.1 %collective-permute-start.1 = (bf16[2,1,16,128]{3,2,1,0:T(8,128)(2,1)S(1)}, bf16[2,1,16,128]{3,2,1,0:T(8,128)(2,1)S(1)}, u32[]{:S(2)}, u32[]{:S(2)}) collective-permute-start(bf16[2,1,16,128]{3,2,1,0:T(8,128)(2,1)S(1)} %collective-permute-done), channel_id=1, source_target_pairs={{0,1},{1,2},{2,3},{3,0},{4,5},{5,6},{6,7},{7,4},{8,9},{9,10},{10,1... | collective-permute-start | bytes 24584 | tf_op jit(solution)/shard_map/ppermute | solution.py:78
  54.7 3.1 %collective-permute-start.2 = (bf16[2,1,16,128]{3,2,1,0:T(8,128)(2,1)S(1)}, bf16[2,1,16,128]{3,2,1,0:T(8,128)(2,1)S(1)}, u32[]{:S(2)}, u32[]{:S(2)}) collective-permute-start(bf16[2,1,16,128]{3,2,1,0:T(8,128)(2,1)S(1)} %collective-permute-done.1), channel_id=1, source_target_pairs={{0,1},{1,2},{2,3},{3,0},{4,5},{5,6},{6,7},{7,4},{8,9},{9,10},{10,1... | collective-permute-start | bytes 24584 | tf_op jit(solution)/shard_map/ppermute | solution.py:78
